TPU v7x, 32 devices: a whole 2x2x4 slice. The times are simulated.
32 devices in a mesh: beam: 2 (over y), tm: 4 (over z), sect: 2 (over x), pol: 2 (over core).
Axes of the slice: x: 2, y: 2, z: 4, core: 2. Of those that a mesh axis runs over, the one named last changes fastest.
Arguments:
- signal: float32 [2, 2, 512, 4096], P(None, 'pol', ('beam', 'tm', 'sect')), parts along dimension 2, may hold values from -6 to 6
- coarse_taps: float32 [16, 4096], replicated, may hold values from -1.5 to 1.5
- fine_taps: float32 [16, 1024], replicated, may hold values from -1.5 to 1.5
- channel_order: int32 [4096], replicated, may hold values from 0 to 4095, each once
Outputs:
- fine_spectra: float32 [2, 2, 8192, 1, 1024], P(None, 'pol', ('beam', 'tm', 'sect')), parts along dimension 2
There are 2 independent parts, one for each index of `beam`. A program takes and returns all parts, laid end to end along the dimension named above; an argument that names none is the same for every part. Nothing has to cross between parts.
Inputs may be any that keep to these rules, and one draw needn't show every extreme that they name: `channel_order`: each of the 4096 coarse channels appears exactly once.
All inputs are finite; a program needn't handle non-finite values.
Results may differ from a plain program's by a relative error of at most 0.0001.
Values sent between devices are 32-bit elements; how exact they have to be, the bound alone decides.
A program may use at most 128 MiB of HBM per device.

v0:
```python
from functools import partial
import math

import jax
import jax.numpy as jnp
from jax import lax
from jax.sharding import PartitionSpec as P


def shifted(value, axis, steps):
    count = lax.axis_size(axis)
    initial, last = (max(0, -steps), min(count, count - steps))
    return lax.ppermute(value, axis, [(source, source + steps) for source in range(initial, last)])


def phase_table(rows, cols, period):
    product_mod = (
        lax.broadcasted_iota(jnp.int32, (rows, cols), 0)
        * lax.broadcasted_iota(jnp.int32, (rows, cols), 1)
        % period
    )
    angles = product_mod.astype(jnp.float32) * (-2.0 * math.pi / period)
    return (jnp.cos(angles), jnp.sin(angles))


def complex_einsum(form, left_re, left_im, right_re, right_im):
    product = partial(jnp.einsum, form, precision=lax.Precision.HIGHEST)
    return (
        product(left_re, right_re) - product(left_im, right_im),
        product(left_re, right_im) + product(left_im, right_re),
    )


def fine_bank(fine_taps, series):
    polars = series.shape[1]
    slots = series.shape[2]
    total_len = series.shape[3]
    tap_count = fine_taps.shape[0]
    fine_width = fine_taps.shape[1]
    frames = -(-total_len // fine_width)
    padded = jnp.pad(
        series, ((0, 0), (0, 0), (0, 0), (0, (frames + tap_count - 1) * fine_width - total_len))
    )
    blocks = padded.reshape(2, polars, slots, frames + tap_count - 1, fine_width)
    filtered = fine_taps[0] * blocks[:, :, :, 0:frames]
    for tap_index in range(1, tap_count):
        filtered = filtered + fine_taps[tap_index] * blocks[:, :, :, tap_index : tap_index + frames]
    table_re, table_im = phase_table(fine_width, fine_width, fine_width)
    out_re, out_im = complex_einsum("pnfj,jm->pnfm", filtered[0], filtered[1], table_re, table_im)
    return jnp.stack([out_re, out_im]) * (1.0 / math.sqrt(fine_width))


def owner_bank(fine_taps, arrived):
    series = jnp.swapaxes(arrived[:, :, :, 0, :], 2, 3)
    return fine_bank(fine_taps, series)


def body(signal, coarse_taps, fine_taps, channel_order):
    polars = signal.shape[1]
    slab_len = signal.shape[2]
    coarse_width = signal.shape[3]
    tap_count = coarse_taps.shape[0]
    lead_rows = signal[:, :, : tap_count - 1, :]
    next_rows = shifted(lead_rows, ("tm", "sect"), -1)
    extended = jnp.concatenate([signal, next_rows], axis=2)
    filtered = coarse_taps[0] * extended[:, :, 0:slab_len, :]
    for tap_index in range(1, tap_count):
        filtered = (
            filtered + coarse_taps[tap_index] * extended[:, :, tap_index : tap_index + slab_len, :]
        )
    factor = math.isqrt(coarse_width)
    shaped = filtered.reshape(2, polars, slab_len, factor, factor)
    base_re, base_im = phase_table(factor, factor, factor)
    twist_re, twist_im = phase_table(factor, factor, coarse_width)
    section_re, section_im = complex_einsum("ptab,ak->ptkb", shaped[0], shaped[1], base_re, base_im)
    turned_re = section_re * twist_re - section_im * twist_im
    turned_im = section_re * twist_im + section_im * twist_re
    spec_re, spec_im = complex_einsum("ptkb,bm->ptmk", turned_re, turned_im, base_re, base_im)
    norm_scale = 1.0 / math.sqrt(coarse_width)
    spectra = jnp.stack([spec_re, spec_im]).reshape(2, polars, slab_len, coarse_width) * norm_scale
    ordered = jnp.take(spectra, channel_order, axis=3)
    owners = lax.axis_size(("tm", "sect"))
    own_count = coarse_width // owners
    blocks = ordered.reshape(2, polars, slab_len, owners, own_count)
    return owner_bank(
        fine_taps, lax.all_to_all(blocks, ("tm", "sect"), split_axis=3, concat_axis=2, tiled=True)
    )


def solution(mesh):
    in_specs = (P(None, "pol", ("beam", "tm", "sect"), None), P(), P(), P())
    out_specs = P(None, "pol", ("beam", "tm", "sect"), None, None)
    return jax.shard_map(body, mesh=mesh, in_specs=in_specs, out_specs=out_specs, check_vma=False)
```

profile of v0, /device:TPU:0, one launch (start us, length us, event | category | flops | bytes accessed | tf_op | source)
XLA Modules:
  0.0 276.9 jit_solution(5803261154416842397)
XLA Ops:
  0.0 0.0 copy-start
  0.0 1.2 slice.209
  1.2 1.3 collective-permute-start
  2.5 0.7 compare_and_fusion
  3.2 0.7 fusion.93
  3.9 0.1 fusion.82
  4.1 2.3 fusion.143
  6.3 0.1 fusion.81
  6.5 0.1 copy.14
  6.6 0.1 copy.15
  6.7 1.3 constant_dynamic-update-slice_fusion.1
  8.0 10.0 %collective-permute-done = f32[2,1,15,4096]{3,2,1,0:T(8,128)S(1)} collective-permute-done((f32[2,1,15,4096]{3,2,1,0:T(8,128)S(1)}, f32[2,1,15,4096]{3,2,1,0:T(8,128)S(1)}, u32[]{:S(2)}, u32[]{:S(2)}) %collective-permute-start) | collective-permute-done | bytes 491552 | tf_op jit(solution)/shard_map/ppermute | solution.py:13
  18.0 0.0 copy-done
  18.0 2.1 fusion.39
  20.1 0.9 fusion.142
  20.9 0.4 reshape.281
  21.4 1.2 fusion.66
  22.5 2.1 fusion.72
  24.7 1.5 reshape.282
  26.1 1.2 fusion.37
  27.3 2.4 fusion.38
  29.7 3.2 %fusion.56 = f32[64,32,64]{2,0,1:T(8,128)S(1)} fusion(f32[64,1,32,64]{3,0,2,1:T(8,128)S(1)} %fusion.37, f32[64,1,32,64]{3,0,2,1:T(8,128)S(1)} %fusion.38, f32[64,64]{1,0:T(8,128)S(1)} %copy.15, f32[64,64]{1,0:T(8,128)S(1)} %copy.14), kind=kOutput, calls=%fused_computation.93 | convolution fusion | flops 101113856 | bytes 1605632 | tf_op jit(solution)/shard_map/ptkb,bm->ptmk/dot_general | solution.py:30
  32.9 3.2 %fusion.58 = f32[64,32,64]{2,0,1:T(8,128)S(1)} fusion(f32[64,1,32,64]{3,0,2,1:T(8,128)S(1)} %fusion.37, f32[64,1,32,64]{3,0,2,1:T(8,128)S(1)} %fusion.38, f32[64,64]{1,0:T(8,128)S(1)} %copy.15, f32[64,64]{1,0:T(8,128)S(1)} %copy.14), kind=kOutput, calls=%fused_computation.95 | convolution fusion | flops 101113856 | bytes 1605632 | tf_op jit(solution)/shard_map/ptkb,bm->ptmk/dot_general | solution.py:29
  36.1 4.2 %fusion.35 = f32[1,32,64,64]{3,2,1,0:T(8,128)} fusion(f32[64,32,64]{2,0,1:T(8,128)S(1)} %fusion.56, f32[64,1,32,64]{3,0,2,1:T(8,128)S(1)} %fusion.37, f32[64,1,32,64]{3,0,2,1:T(8,128)S(1)} %fusion.38, f32[64,64]{1,0:T(8,128)S(1)} %copy.15, f32[64,64]{1,0:T(8,128)S(1)} %copy.14), kind=kOutput, calls=%fused_computation.53 | convolution fusion | flops 101244928 | bytes 2129920 | tf_op jit(solution)/shard_map/ptkb,bm->ptmk/dot_general | solution.py:30
  52.3 2.4 stack.19
  54.7 4.2 %fusion.36 = f32[1,32,64,64]{3,2,1,0:T(8,128)} fusion(f32[64,32,64]{2,0,1:T(8,128)S(1)} %fusion.58, f32[64,1,32,64]{3,0,2,1:T(8,128)S(1)} %fusion.37, f32[64,1,32,64]{3,0,2,1:T(8,128)S(1)} %fusion.38, f32[64,64]{1,0:T(8,128)S(1)} %copy.15, f32[64,64]{1,0:T(8,128)S(1)} %copy.14), kind=kOutput, calls=%fused_computation.55 | convolution fusion | flops 101244928 | bytes 2129920 | tf_op jit(solution)/shard_map/ptkb,bm->ptmk/dot_general | solution.py:29
  58.9 1.6 stack.18
  60.4 1.1 maximum_multiply_fusion.1
  61.6 4.4 %copy.20 = f32[2,1,32,4096]{2,0,3,1:T(2,128)} copy(f32[2,1,32,4096]{3,2,1,0:T(8,128)S(1)} %maximum_multiply_fusion.1) | data formatting | bytes 2097152
  65.9 30.5 %gather_fusion = f32[4096,2,32]{2,1,0:T(2,128)} fusion(f32[2,32,4096]{1,0,2:T(2,128)} %bitcast.116, s32[4096]{0:T(1024)S(1)} %fusion.93), kind=kCustom, calls=%fused_computation | custom fusion | bytes 2113536 | tf_op jit(solution)/shard_map/jit(_take)/gather | solution.py:81
  96.4 0.0 copy-start.1
  96.4 5.2 %copy.17 = f32[2,1,32,8,512]{4,2,0,1,3:T(8,128)S(1)} copy(f32[2,1,32,8,512]{2,0,4,3,1:T(2,128)} %bitcast.117) | data formatting | bytes 2097152 | tf_op jit(solution)/shard_map/jit(_take)/gather | solution.py:81
  101.6 1.1 broadcast_select_fusion
  102.7 5.9 %all-to-all-start = ((f32[2,1,32,8,512]{4,2,0,1,3:T(8,128)}), f32[2,1,32,8,512]{4,2,0,1,3:T(8,128)S(1)}, u32[]{:S(2)}, u32[]{:S(2)}) async-start(f32[2,1,32,8,512]{4,2,0,1,3:T(8,128)} %broadcast_select_fusion), calls=%async_computation | async-start | bytes 2097152 | tf_op jit(solution)/shard_map/all_to_all | solution.py:86
  108.6 0.0 copy-done.1
  108.7 25.1 %all-to-all-done = f32[2,1,32,8,512]{4,2,0,1,3:T(8,128)S(1)} async-done(((f32[2,1,32,8,512]{4,2,0,1,3:T(8,128)}), f32[2,1,32,8,512]{4,2,0,1,3:T(8,128)S(1)}, u32[]{:S(2)}, u32[]{:S(2)}) %all-to-all-start) | async-done | bytes 1048608 | tf_op jit(solution)/shard_map/all_to_all | solution.py:86
  133.8 0.1 copy.18
  133.9 21.3 %pad.4 = f32[2,1,512,16384]{2,3,0,1:T(8,128)} pad(f32[2,1,512,256]{2,3,0,1:T(8,128)S(1)} %bitcast.118, f32[]{:T(128)} %constant.61.clone.1), padding=0_0x0_0x0_0x0_16128 | pad | bytes 68157440 | tf_op jit(solution)/shard_map/jit(_pad)/pad | solution.py:41
  155.2 21.7 %fusion.3 = f32[2,1,512,1,1024]{2,4,3,0,1:T(8,128)S(1)} fusion(f32[2,1,512,16,1024]{2,4,3,0,1:T(8,128)} %bitcast.38, f32[1024]{0:T(1024)S(1)} %bitcast.149, f32[1024]{0:T(1024)S(1)} %bitcast.150, f32[1024]{0:T(1024)S(1)} %bitcast.136, f32[1024]{0:T(1024)S(1)} %bitcast.137, f32[1024]{0:T(1024)S(1)} %bitcast.138, f32[1024]{0:T(1024)S(1)} %bitcast.139, ...), kind=kLoop, calls=%fused_computation.8 | loop fusion | flops 32505856 | bytes 71368704 | tf_op jit(solution)/shard_map/add | solution.py:47
  176.9 22.8 %fusion.23 = f32[512,1024]{1,0:T(8,128)S(1)} fusion(f32[2,1,512,1,1024]{2,4,3,0,1:T(8,128)S(1)} %fusion.3), kind=kOutput, calls=%fused_computation.48 | convolution fusion | flops 6457131008 | bytes 4194304 | tf_op jit(solution)/shard_map/pnfj,jm->pnfm/dot_general | solution.py:30
  199.8 23.2 %fusion.25 = f32[512,1024]{1,0:T(8,128)S(1)} fusion(f32[2,1,512,1,1024]{2,4,3,0,1:T(8,128)S(1)} %fusion.3), kind=kOutput, calls=%fused_computation.49 | convolution fusion | flops 6457131008 | bytes 4194304 | tf_op jit(solution)/shard_map/pnfj,jm->pnfm/dot_general | solution.py:29
  223.0 23.2 %add_bitcast_fusion = f32[1,1,512,1,1024]{4,2,3,1,0:T(8,128)S(1)} fusion(f32[512,1024]{1,0:T(8,128)S(1)} %fusion.23, f32[2,1,512,1,1024]{2,4,3,0,1:T(8,128)S(1)} %fusion.3), kind=kOutput, calls=%fused_computation.44 | convolution fusion | flops 6457655296 | bytes 6291456 | tf_op jit(solution)/shard_map/pnfj,jm->pnfm/dot_general | solution.py:30
  246.2 23.5 %subtract_bitcast_fusion = f32[1,1,512,1,1024]{4,2,3,1,0:T(8,128)S(1)} fusion(f32[512,1024]{1,0:T(8,128)S(1)} %fusion.25, f32[2,1,512,1,1024]{2,4,3,0,1:T(8,128)S(1)} %fusion.3), kind=kOutput, calls=%fused_computation.45 | convolution fusion | flops 6457655296 | bytes 6291456 | tf_op jit(solution)/shard_map/pnfj,jm->pnfm/dot_general | solution.py:29
  269.7 0.4 maximum_multiply_fusion
  270.1 6.3 %copy.19 = f32[2,1,512,1,1024]{4,3,2,1,0:T(1,128)} copy(f32[2,1,512,1,1024]{4,2,3,1,0:T(8,128)S(1)} %maximum_multiply_fusion) | data formatting | bytes 8388608 | tf_op jit(solution)/shard_map/mul | solution.py:50
  (3 shorter events, 0.1 us)
Async XLA Ops:
  0.0 18.0 %copy-start = (f32[2,1,32,4096]{3,2,1,0:T(8,128)S(1)}, f32[2,1,32,4096]{3,2,1,0:T(8,128)}, u32[]{:S(2)}) copy-start(f32[2,1,32,4096]{3,2,1,0:T(8,128)} %param.4) | copy-start | bytes 3145732
  1.2 16.8 %collective-permute-start = (f32[2,1,15,4096]{3,2,1,0:T(8,128)S(1)}, f32[2,1,15,4096]{3,2,1,0:T(8,128)S(1)}, u32[]{:S(2)}, u32[]{:S(2)}) collective-permute-start(f32[2,1,15,4096]{3,2,1,0:T(8,128)S(1)} %slice.209), channel_id=1, source_target_pairs={{2,0},{4,2},{6,4},{8,6},{10,8},{12,10},{14,12},{3,1},{5,3},{7,5},{... | collective-permute-start | bytes 1474568 | tf_op jit(solution)/shard_map/ppermute | solution.py:13
  96.4 12.3 %copy-start.1 = (f32[16,1024]{1,0:T(8,128)S(1)}, f32[16,1024]{1,0:T(8,128)}, u32[]{:S(2)}) copy-start(f32[16,1024]{1,0:T(8,128)} %param.6) | copy-start | bytes 196612
  102.7 31.1 %all-to-all-start = ((f32[2,1,32,8,512]{4,2,0,1,3:T(8,128)}), f32[2,1,32,8,512]{4,2,0,1,3:T(8,128)S(1)}, u32[]{:S(2)}, u32[]{:S(2)}) async-start(f32[2,1,32,8,512]{4,2,0,1,3:T(8,128)} %broadcast_select_fusion), calls=%async_computation | async-start | bytes 2097152 | tf_op jit(solution)/shard_map/all_to_all | solution.py:86
where the time goes:
time: 281 us; the launch traced here: 277 us
  matrix products  114 us (41%)
  local copies, waits for them, and re-layouts  79.4 us (28%)
  waiting for transfers between devices  35 us (12%)
  other arithmetic  28.2 us (10%)
  between operations  12.6 us (4%)
  starting transfers between devices  7.22 us (3%)
    gather x2, local copies, waits for them, and re-layouts, body(): ordered = jnp.take(spectra, channel_order, axis=3)  35.6 us
    dot_general x3, matrix products, complex_einsum(): product(left_im, right_im)  30 us
    dot_general x3, matrix products, complex_einsum(): product(left_re, right_re) - product(left_im, right_im)  28.6 us
    dot_general x3, matrix products, complex_einsum(): product(left_im, right_re)  28.2 us
    dot_general x3, matrix products, complex_einsum(): product(left_re, right_im) + product(left_im, right_re)  27.6 us
    all_to_all x1, waiting for transfers between devices, body(): lax.all_to_all(blocks, ('tm', 'sect'), split_axis=3, concat_axis=2, tiled...  25.1 us
    add x1, other arithmetic, fine_bank(): filtered + fine_taps[tap_index] * blocks[:, :, :, tap_index:tap_index + f...  21.7 us
    pad x1, local copies, waits for them, and re-layouts, fine_bank(): jnp.pad(series, ((0, 0), (0, 0), (0, 0), (0, (frames + tap_count - 1) * f...  21.3 us
  transfers between devices with their start and end apart: 2, of which 2 were waited for; matrix products, arithmetic and copies ran while one was open for 2% of the time, Pallas kernels for 0%

commit v1 on v0

v1 whole, which is shorter than its diff:
```python
from functools import partial
import math

import jax
import jax.numpy as jnp
import numpy as np
from jax import lax
from jax.experimental import pallas as pl
from jax.experimental.pallas import tpu as pltpu
from jax.sharding import PartitionSpec as P

LANES = 128
ROWS = 8
GROUP = ("tm", "sect")


def shifted(value, axis, steps):
    count = lax.axis_size(axis)
    initial, last = (max(0, -steps), min(count, count - steps))
    return lax.ppermute(value, axis, [(source, source + steps) for source in range(initial, last)])


def split_const(table):
    high = np.asarray(table, np.float32).astype(jnp.bfloat16)
    low = (np.asarray(table, np.float64) - high.astype(np.float64)).astype(jnp.bfloat16)
    return high, low


def split(value):
    high = value.astype(jnp.bfloat16)
    low = (value - high.astype(jnp.float32)).astype(jnp.bfloat16)
    return high, low


def dot3(high, low, table_high, table_low):
    product = partial(jnp.dot, preferred_element_type=jnp.float32)
    return product(high, table_high) + (product(low, table_high) + product(high, table_low))


def butterflies(points):
    count = len(points)
    if count == 1:
        return points
    even, odd = butterflies(points[0::2]), butterflies(points[1::2])
    first, second = [], []
    for k in range(count // 2):
        angle = -2.0 * math.pi * k / count
        cos, sin = math.cos(angle), math.sin(angle)
        (er, ei), (xr, xi) = even[k], odd[k]
        if k == 0:
            tr, ti = xr, xi
        elif 4 * k == count:
            tr, ti = xi, -xr
        else:
            tr, ti = xr * cos - xi * sin, xr * sin + xi * cos
        first.append((er + tr, ei + ti))
        second.append((er - tr, ei - ti))
    return first + second


def coarse_tables(width):
    chunks = width // LANES
    k, b = np.arange(chunks)[:, None], np.arange(LANES)[None, :]
    angle = 2.0 * np.pi * (k * b % width) / width
    twist = np.stack([np.cos(angle), -np.sin(angle)]).astype(np.float32)
    b, m = np.arange(LANES)[:, None], np.arange(LANES)[None, :]
    angle = 2.0 * np.pi * (b * m % LANES) / LANES
    cos, sin = np.cos(angle), np.sin(angle)
    matrix = np.block([[cos, -sin], [sin, cos]]) / math.sqrt(width)
    high, low = split_const(matrix)
    return twist, high, low


def fill(ext, source, first_row):
    chunks = ext.shape[1]
    rows = source.shape[1]
    for q in range(chunks):
        for c in range(2):
            ext[c, q, first_row : first_row + rows, :] = source[c, :, q * LANES : (q + 1) * LANES]


def spectra_rows(ext, taps_ref, twist_ref, high_ref, low_ref, filt, lhs, spec, start, rows):
    chunks = ext.shape[1]
    tap_count = taps_ref.shape[0]
    groups = rows // ROWS

    @pl.loop(0, chunks)
    def _(q):
        lanes = pl.ds(pl.multiple_of(q * LANES, LANES), LANES)
        sums = [[None] * groups for _ in range(2)]
        for k in range(tap_count):
            tap = jnp.broadcast_to(taps_ref[k : k + 1, lanes], (ROWS, LANES))
            for c in range(2):
                for g in range(groups):
                    term = tap * ext[c, q, start + g * ROWS + k : start + (g + 1) * ROWS + k, :]
                    sums[c][g] = term if k == 0 else sums[c][g] + term
        for c in range(2):
            for g in range(groups):
                filt[c, q, start + g * ROWS : start + (g + 1) * ROWS, :] = sums[c][g]

    @pl.loop(0, groups)
    def _(g):
        at = pl.ds(pl.multiple_of(start + g * ROWS, ROWS), ROWS)
        points = [(filt[0, q, at, :], filt[1, q, at, :]) for q in range(chunks)]
        for k, (re, im) in enumerate(butterflies(points)):
            wr, wi = twist_ref[0, k : k + 1, :], twist_ref[1, k : k + 1, :]
            lhs[k, at, 0:LANES] = re * wr - im * wi
            lhs[k, at, LANES : 2 * LANES] = re * wi + im * wr

    @pl.loop(0, chunks // 8)
    def _(j):
        part = pl.ds(j * 8, 8)
        value = lhs[part, start : start + rows, :].reshape(8 * rows, 2 * LANES)
        high, low = split(value)
        result = dot3(high, low, high_ref[...], low_ref[...])
        spec[part, start : start + rows, :] = result.reshape(8, rows, 2 * LANES)


def gathered(spec, place_ref, p, start, rows):
    chunks = spec.shape[0]
    place = jnp.broadcast_to(place_ref[pl.ds(p, 1), :], (ROWS, LANES))
    lane = place % LANES
    chunk = place // LANES
    keys = [(c, g) for c in range(2) for g in range(rows // ROWS)]
    sums = {}
    for q in range(chunks):
        mask = chunk == q
        for c, g in keys:
            source = spec[q, start + g * ROWS : start + (g + 1) * ROWS, c * LANES : (c + 1) * LANES]
            moved = jnp.take_along_axis(source, lane, axis=1, mode="promise_in_bounds")
            sums[c, g] = moved if q == 0 else jnp.where(mask, moved, sums[c, g])
    return sums


def coarse_kernel(signal_ref, next_ref, taps_ref, place_ref, twist_ref, high_ref, low_ref, out_ref, ext, filt, lhs, spec):
    rows = signal_ref.shape[1]
    fill(ext, signal_ref, 0)
    fill(ext, next_ref, rows)
    spectra_rows(ext, taps_ref, twist_ref, high_ref, low_ref, filt, lhs, spec, 0, rows)
    chunks = spec.shape[0]

    @pl.loop(0, chunks)
    def _(p):
        sums = gathered(spec, place_ref, p, 0, rows)
        for (c, g), value in sums.items():
            out_ref[p, c, g * ROWS : (g + 1) * ROWS, :] = value


def coarse_local(signal, next_rows, taps, place):
    _, rows, width = signal.shape
    chunks = width // LANES
    twist, high, low = coarse_tables(width)
    lead = next_rows.shape[1]
    return pl.pallas_call(
        coarse_kernel,
        out_shape=jax.ShapeDtypeStruct((chunks, 2, rows, LANES), jnp.float32),
        in_specs=[pl.BlockSpec(memory_space=pltpu.VMEM)] * 7,
        out_specs=pl.BlockSpec(memory_space=pltpu.VMEM),
        scratch_shapes=[
            pltpu.VMEM((2, chunks, rows + lead, LANES), jnp.float32),
            pltpu.VMEM((2, chunks, rows, LANES), jnp.float32),
            pltpu.VMEM((chunks, rows, 2 * LANES), jnp.float32),
            pltpu.VMEM((chunks, rows, 2 * LANES), jnp.float32),
        ],
        name="coarse",
    )(signal, next_rows, taps, place, twist, high, low)


def fine_kernel(arrived_ref, taps_ref, cos_high, cos_low, sin_high, sin_low, out_ref):
    sources, slot_chunks, _, rows, slots = arrived_ref.shape
    length = sources * rows
    width = cos_high.shape[1]
    high, low = [], []
    for c in range(2):
        series = arrived_ref[:, 0, c].reshape(length, slots)
        filtered = series.T * taps_ref[...]
        parts = split(filtered)
        high.append(parts[0])
        low.append(parts[1])
    high = jnp.concatenate(high, axis=0)
    low = jnp.concatenate(low, axis=0)
    per_slot = width // LANES
    step = 2 * LANES
    for m in range(width // step):
        lanes = slice(m * step, (m + 1) * step)
        with_cos = dot3(high, low, cos_high[:, lanes], cos_low[:, lanes])
        with_sin = dot3(high, low, sin_high[:, lanes], sin_low[:, lanes])
        re = with_cos[:slots] + with_sin[slots:]
        im = with_cos[slots:] - with_sin[:slots]
        for h in range(2):
            at = pl.ds(m * 2 + h, slots, stride=per_slot)
            out_ref[0, at, :] = re[:, h * LANES : (h + 1) * LANES]
            out_ref[1, at, :] = im[:, h * LANES : (h + 1) * LANES]


def fine_local(arrived, fine_taps):
    sources, slot_chunks, _, rows, slots = arrived.shape
    length = sources * rows
    width = fine_taps.shape[1]
    j, m = np.arange(length)[:, None], np.arange(width)[None, :]
    angle = 2.0 * np.pi * (j * m % width) / width
    scale = 1.0 / math.sqrt(width)
    tables = split_const(np.cos(angle) * scale) + split_const(np.sin(angle) * scale)
    per_slot = width // LANES
    whole = lambda shape: pl.BlockSpec(shape, lambda i: (0, 0))
    out = pl.pallas_call(
        fine_kernel,
        grid=(slot_chunks,),
        out_shape=jax.ShapeDtypeStruct((2, slot_chunks * slots * per_slot, LANES), jnp.float32),
        in_specs=[
            pl.BlockSpec((sources, 1, 2, rows, slots), lambda i: (0, i, 0, 0, 0)),
            whole((1, length)),
        ]
        + [whole((length, width))] * 4,
        out_specs=pl.BlockSpec((2, slots * per_slot, LANES), lambda i: (0, i, 0)),
        name="fine",
    )(arrived, fine_taps[0:1, :length], *tables)
    return out.reshape(2, 1, slot_chunks * slots, 1, width)


def fine_general(series, fine_taps):
    slots, total_len = series.shape[1:]
    tap_count, width = fine_taps.shape
    frames = -(-total_len // width)
    blocks = jnp.pad(series, ((0, 0), (0, 0), (0, frames * width - total_len)))
    blocks = blocks.reshape(2, slots, frames, width)
    filtered = fine_taps[0] * blocks
    for k in range(1, min(tap_count, frames)):
        term = fine_taps[k] * blocks[:, :, k:]
        filtered = filtered + jnp.pad(term, ((0, 0), (0, 0), (0, k), (0, 0)))
    j, m = np.arange(width)[:, None], np.arange(width)[None, :]
    angle = 2.0 * np.pi * (j * m % width) / width
    scale = 1.0 / math.sqrt(width)
    cos = jnp.asarray((np.cos(angle) * scale).astype(np.float32))
    sin = jnp.asarray((np.sin(angle) * scale).astype(np.float32))
    product = partial(jnp.einsum, "snfj,jm->snfm", precision=lax.Precision.HIGHEST)
    with_cos, with_sin = product(filtered, cos), product(filtered, sin)
    return jnp.stack([with_cos[0] + with_sin[1], with_cos[1] - with_sin[0]])[:, None]


def body(signal, coarse_taps, fine_taps, channel_order):
    signal = signal[:, 0]
    slab_len, width = signal.shape[1:]
    tap_count = coarse_taps.shape[0]
    chunks = width // LANES
    owners = lax.axis_size(GROUP)
    own_count = width // owners
    place = (channel_order % chunks * LANES + channel_order // chunks).reshape(chunks, LANES)
    lead = -(-(tap_count - 1) // ROWS) * ROWS
    next_rows = shifted(signal[:, :lead], GROUP, -1)
    ordered = coarse_local(signal, next_rows, coarse_taps, place)
    total_len = owners * slab_len
    if own_count % LANES == 0 and total_len <= fine_taps.shape[1]:
        blocks = ordered.reshape(owners, own_count // LANES, 2, slab_len, LANES)
        arrived = lax.all_to_all(blocks, GROUP, split_axis=0, concat_axis=0, tiled=True)
        return fine_local(arrived, fine_taps)
    blocks = ordered.transpose(0, 3, 1, 2).reshape(owners, own_count, 2, slab_len)
    arrived = lax.all_to_all(blocks, GROUP, split_axis=0, concat_axis=0, tiled=True)
    series = arrived.transpose(2, 1, 0, 3).reshape(2, own_count, total_len)
    return fine_general(series, fine_taps)


def solution(mesh):
    in_specs = (P(None, "pol", ("beam", "tm", "sect"), None), P(), P(), P())
    out_specs = P(None, "pol", ("beam", "tm", "sect"), None, None)
    return jax.shard_map(body, mesh=mesh, in_specs=in_specs, out_specs=out_specs, check_vma=False)
```

time: 281 us -> 74.9 us (0.27); the launches traced: 277 us -> 74.5 us
  matrix products: 114 us -> 0 us
  local copies, waits for them, and re-layouts: 79.4 us -> 4.11 us
  other arithmetic: 28.2 us -> 1.34 us
  Pallas kernels: 0 us -> 23.8 us
  between operations: 12.6 us -> 0.02 us
  waiting for transfers between devices: 35 us -> 38 us
    dot_general x12 -> x0, matrix products: 114 us -> none  [the longest x3 30 us: complex_einsum(): product(left_im, right_im)]
    gather x2 -> x0, local copies, waits for them, and re-layouts: 35.6 us -> none  [body(): ordered = jnp.take(spectra, channel_order, axis=3)]
    add x2 -> x0, other arithmetic: 23.8 us -> none  [the longest x1 21.7 us: fine_bank(): filtered + fine_taps[tap_index] * blocks[:, :, :, tap_index:tap_index + f...]
    pallas_call x0 -> x2, Pallas kernels: none -> 23.8 us  [the longest x1 16.7 us: coarse_local(): pl.pallas_call(coarse_kernel, out_shape=jax.ShapeDtypeStruct((chunks, 2,...]
    pad x1 -> x0, local copies, waits for them, and re-layouts: 21.3 us -> none  [fine_bank(): jnp.pad(series, ((0, 0), (0, 0), (0, 0), (0, (frames + tap_count - 1) * f...]
    mul x1 -> x0, local copies, waits for them, and re-layouts: 6.33 us -> none  [fine_bank(): return jnp.stack([out_re, out_im]) * (1.0 / math.sqrt(fine_width))]
    another operation x4 -> x0, local copies, waits for them, and re-layouts: 5.81 us -> none  [the longest x2 3.95 us: body(): jnp.stack([spec_re, spec_im]).reshape(2, polars, slab_len, coarse_width)]
    ppermute x1, waiting for transfers between devices: 9.97 us -> 14.2 us  [shifted(): lax.ppermute(value, axis, [(source, source + steps) for source in range(i...]
  transfers between devices with their start and end apart: 2 -> 2, of which waited for: 2 -> 2; matrix products, arithmetic and copies ran while one was open for 2% -> 4% of each run, Pallas kernels for 0% -> 0%
where the time goes in v1:
time: 74.9 us; the launch traced here: 74.5 us
  waiting for transfers between devices  38 us (51%)
  Pallas kernels  23.8 us (32%)
  starting transfers between devices  7.22 us (10%)
  local copies, waits for them, and re-layouts  4.11 us (5%)
  other arithmetic  1.34 us (2%)
    all_to_all x1, waiting for transfers between devices, body(): lax.all_to_all(blocks, GROUP, split_axis=0, concat_axis=0, tiled=True)  23.9 us
    pallas_call x1, Pallas kernels, coarse_local(): pl.pallas_call(coarse_kernel, out_shape=jax.ShapeDtypeStruct((chunks, 2,...  16.7 us
    ppermute x1, waiting for transfers between devices, shifted(): lax.ppermute(value, axis, [(source, source + steps) for source in range(i...  14.2 us
    pallas_call x1, Pallas kernels, fine_local(): pl.pallas_call(fine_kernel, grid=(slot_chunks,), out_shape=jax.ShapeDtype...  7.05 us
    all_to_all x1, starting transfers between devices, body(): lax.all_to_all(blocks, GROUP, split_axis=0, concat_axis=0, tiled=True)  5.93 us
    unnamed x4, local copies, waits for them, and re-layouts  1.76 us
  transfers between devices with their start and end apart: 2, of which 2 were waited for; matrix products, arithmetic and copies ran while one was open for 4% of the time, Pallas kernels for 0%

profile of v1, /device:TPU:0, one launch (start us, length us, event | category | flops | bytes accessed | tf_op | source)
XLA Modules:
  0.0 74.5 jit_solution(986165995002598730)
XLA Ops:
  0.0 1.1 %slice.8 = f32[2,16,4096]{2,1,0:T(8,128)S(1)} slice(f32[2,32,4096]{2,1,0:T(8,128)} %bitcast.6), slice={[0:2], [0:16], [0:4096]} | slice | bytes 1048576 | tf_op jit(solution)/shard_map/slice | solution.py:250
  1.1 1.3 %collective-permute-start = (f32[2,16,4096]{2,1,0:T(8,128)S(1)}, f32[2,16,4096]{2,1,0:T(8,128)S(1)}, u32[]{:S(2)}, u32[]{:S(2)}) collective-permute-start(f32[2,16,4096]{2,1,0:T(8,128)S(1)} %slice.8), channel_id=1, source_target_pairs={{2,0},{4,2},{6,4},{8,6},{10,8},{12,10},{14,12},{3,1},{5,3},{7,5},{... | collective-permute-start | bytes 1572872 | tf_op jit(solution)/shard_map/ppermute | solution.py:20
  2.4 1.3 %fusion.2.place_ref = s32[32,128]{1,0:T(8,128)} fusion(s32[4096]{0:T(1024)} %param.14), kind=kLoop, calls=%fused_computation.7 | loop fusion | flops 86016 | bytes 32768 | tf_op jit(solution)/shard_map/reshape | solution.py:248
  3.7 14.2 %collective-permute-done.next_ref = f32[2,16,4096]{2,1,0:T(8,128)S(1)} collective-permute-done((f32[2,16,4096]{2,1,0:T(8,128)S(1)}, f32[2,16,4096]{2,1,0:T(8,128)S(1)}, u32[]{:S(2)}, u32[]{:S(2)}) %collective-permute-start) | collective-permute-done | bytes 524320 | tf_op jit(solution)/shard_map/ppermute | solution.py:20
  17.9 0.0 copy-start.1
  17.9 0.8 %copy-done.1 = f32[2,16,4096]{2,1,0:T(8,128)} copy-done((f32[2,16,4096]{2,1,0:T(8,128)}, f32[2,16,4096]{2,1,0:T(8,128)S(1)}, u32[]{:S(2)}) %copy-start.1) | copy-done | bytes 524312
  18.7 16.7 %coarse.1 = f32[32,2,32,128]{3,2,1,0:T(8,128)} custom-call(f32[2,32,4096]{2,1,0:T(8,128)} %bitcast.7, f32[2,16,4096]{2,1,0:T(8,128)} %copy-done.1, f32[16,4096]{1,0:T(8,128)} %taps_ref.1, s32[32,128]{1,0:T(8,128)} %fusion.2.place_ref, f32[2,32,128]{2,1,0:T(8,128)} %constant.44.clone.twist_ref, bf16[256,256]{1,0:T(8,128)(2,1)} %constant.45.clone.high_ref, ...), custom_call_target="tpu_custom_call" | custom-call | tf_op jit(solution)/shard_map/coarse/pallas_call | solution.py:154
  35.4 5.9 %all-to-all-start = ((f32[8,4,2,32,128]{4,3,2,1,0:T(8,128)}), f32[8,4,2,32,128]{4,3,2,1,0:T(8,128)S(1)}, u32[]{:S(2)}, u32[]{:S(2)}) async-start(f32[8,4,2,32,128]{4,3,2,1,0:T(8,128)} %bitcast.5), calls=%async_computation | async-start | bytes 2097152 | tf_op jit(solution)/shard_map/all_to_all | solution.py:255
  41.3 1.3 %slice.7.taps_ref = f32[1,256]{1,0:T(1,128)} slice(f32[16,1024]{1,0:T(8,128)} %param.13), slice={[0:1], [0:256]} | slice | bytes 2048 | tf_op jit(solution)/shard_map/slice | solution.py:217
  42.6 23.9 %all-to-all-done.arrived_ref = f32[8,4,2,32,128]{4,3,2,1,0:T(8,128)S(1)} async-done(((f32[8,4,2,32,128]{4,3,2,1,0:T(8,128)}), f32[8,4,2,32,128]{4,3,2,1,0:T(8,128)S(1)}, u32[]{:S(2)}, u32[]{:S(2)}) %all-to-all-start) | async-done | bytes 1048608 | tf_op jit(solution)/shard_map/all_to_all | solution.py:255
  66.5 0.0 copy-start
  66.5 1.0 %copy-done = f32[8,4,2,32,128]{4,3,2,1,0:T(8,128)} copy-done((f32[8,4,2,32,128]{4,3,2,1,0:T(8,128)}, f32[8,4,2,32,128]{4,3,2,1,0:T(8,128)S(1)}, u32[]{:S(2)}) %copy-start) | copy-done | bytes 1048600
  67.4 7.0 %fine.1 = f32[2,4096,128]{2,1,0:T(8,128)} custom-call(f32[8,4,2,32,128]{4,3,2,1,0:T(8,128)} %copy-done, f32[1,256]{1,0:T(1,128)} %slice.7.taps_ref, bf16[256,1024]{1,0:T(8,128)(2,1)} %constant.47.clone.cos_high, bf16[256,1024]{1,0:T(8,128)(2,1)} %constant.48.clone.cos_low, bf16[256,1024]{1,0:T(8,128)(2,1)} %constant.49.clone.sin_high, ...), custom_call_target="tpu_custom_call" | custom-call | tf_op jit(solution)/shard_map/fine/pallas_call | solution.py:206
Async XLA Ops:
  1.1 16.8 %collective-permute-start = (f32[2,16,4096]{2,1,0:T(8,128)S(1)}, f32[2,16,4096]{2,1,0:T(8,128)S(1)}, u32[]{:S(2)}, u32[]{:S(2)}) collective-permute-start(f32[2,16,4096]{2,1,0:T(8,128)S(1)} %slice.8), channel_id=1, source_target_pairs={{2,0},{4,2},{6,4},{8,6},{10,8},{12,10},{14,12},{3,1},{5,3},{7,5},{... | collective-permute-start | bytes 1572872 | tf_op jit(solution)/shard_map/ppermute | solution.py:20
  17.9 0.8 %copy-start.1 = (f32[2,16,4096]{2,1,0:T(8,128)}, f32[2,16,4096]{2,1,0:T(8,128)S(1)}, u32[]{:S(2)}) copy-start(f32[2,16,4096]{2,1,0:T(8,128)S(1)} %collective-permute-done.next_ref) | copy-start | bytes 1572868
  35.4 31.1 %all-to-all-start = ((f32[8,4,2,32,128]{4,3,2,1,0:T(8,128)}), f32[8,4,2,32,128]{4,3,2,1,0:T(8,128)S(1)}, u32[]{:S(2)}, u32[]{:S(2)}) async-start(f32[8,4,2,32,128]{4,3,2,1,0:T(8,128)} %bitcast.5), calls=%async_computation | async-start | bytes 2097152 | tf_op jit(solution)/shard_map/all_to_all | solution.py:255
  66.5 1.0 %copy-start = (f32[8,4,2,32,128]{4,3,2,1,0:T(8,128)}, f32[8,4,2,32,128]{4,3,2,1,0:T(8,128)S(1)}, u32[]{:S(2)}) copy-start(f32[8,4,2,32,128]{4,3,2,1,0:T(8,128)S(1)} %all-to-all-done.arrived_ref) | copy-start | bytes 3145732

commit v2 on v1

--- a/solution.py
+++ b/solution.py
@@ -12,6 +12,7 @@
 LANES = 128
 ROWS = 8
 GROUP = ("tm", "sect")
+PHASES = 2
 
 
 def shifted(value, axis, steps):
@@ -118,9 +119,9 @@
 
 def gathered(spec, place_ref, p, start, rows):
     chunks = spec.shape[0]
-    place = jnp.broadcast_to(place_ref[pl.ds(p, 1), :], (ROWS, LANES))
-    lane = place % LANES
-    chunk = place // LANES
+    channel = jnp.broadcast_to(place_ref[pl.ds(p, 1), :], (ROWS, LANES))
+    lane = lax.div(channel, chunks)
+    chunk = channel - lane * chunks
     keys = [(c, g) for c in range(2) for g in range(rows // ROWS)]
     sums = {}
     for q in range(chunks):
@@ -166,6 +167,133 @@
     )(signal, next_rows, taps, place, twist, high, low)
 
 
+def exchange_kernel(
+    signal_ref, taps_ref, place_ref, twist_ref, high_ref, low_ref, out_ref,
+    halo, ext, filt, lhs, spec, stage, halo_send, halo_recv, send_sem, recv_sem, own_sem,
+):
+    tms, sects = lax.axis_size("tm"), lax.axis_size("sect")
+    owners = tms * sects
+    tm, sect = lax.axis_index("tm"), lax.axis_index("sect")
+    me = tm * sects + sect
+    chunks = spec.shape[0]
+    slot_chunks = chunks // owners
+    slab_len = signal_ref.shape[1]
+    rows = slab_len // PHASES
+    lead = halo.shape[1]
+
+    def device(index):
+        return {"tm": lax.div(index, sects), "sect": lax.rem(index, sects)}
+
+    barrier = pltpu.get_barrier_semaphore()
+    for offset in range(1, owners):
+        peer = lax.rem(me + offset, owners)
+        pl.semaphore_signal(barrier, inc=1, device_id=device(peer), device_id_type=pl.DeviceIdType.MESH)
+    pl.semaphore_wait(barrier, owners - 1)
+
+    halo_copy = pltpu.make_async_remote_copy(
+        src_ref=signal_ref.at[:, 0:lead, :],
+        dst_ref=halo,
+        send_sem=halo_send,
+        recv_sem=halo_recv,
+        device_id=device(lax.rem(me + owners - 1, owners)),
+        device_id_type=pl.DeviceIdType.MESH,
+    )
+
+    @pl.when(me > 0)
+    def _():
+        halo_copy.start()
+
+    def block_copy(phase, owner, source):
+        return pltpu.make_async_remote_copy(
+            src_ref=stage.at[owner, phase],
+            dst_ref=out_ref.at[source, phase],
+            send_sem=send_sem.at[phase, owner],
+            recv_sem=recv_sem.at[phase, source],
+            device_id=device(owner),
+            device_id_type=pl.DeviceIdType.MESH,
+        )
+
+    fill(ext, signal_ref, 0)
+    for phase in range(PHASES):
+        start = phase * rows
+        if phase == PHASES - 1:
+
+            @pl.when(me < owners - 1)
+            def _():
+                halo_copy.wait_recv()
+                fill(ext, halo, slab_len)
+
+            @pl.when(me == owners - 1)
+            def _():
+                ext[:, :, slab_len:, :] = jnp.zeros((2, chunks, lead, LANES), jnp.float32)
+
+        spectra_rows(ext, taps_ref, twist_ref, high_ref, low_ref, filt, lhs, spec, start, rows)
+
+        @pl.loop(0, owners)
+        def _(step):
+            turn = lax.div(step, sects)
+            half = tms // 2
+            turn = jnp.where(turn < tms - half, half + turn, tms - 1 - turn)
+            owner = lax.rem(tm + turn, tms) * sects + lax.rem(sect + 1 + step, sects)
+
+            @pl.loop(0, slot_chunks)
+            def _(i):
+                sums = gathered(spec, place_ref, owner * slot_chunks + i, start, rows)
+                for (c, g), value in sums.items():
+                    stage[owner, phase, i, c, g * ROWS : (g + 1) * ROWS, :] = value
+
+            @pl.when(owner != me)
+            def _():
+                block_copy(phase, owner, me).start()
+
+    own_copy = pltpu.make_async_copy(stage.at[me], out_ref.at[me], own_sem)
+    own_copy.start()
+    own_copy.wait()
+
+    @pl.when(me > 0)
+    def _():
+        halo_copy.wait_send()
+
+    for phase in range(PHASES):
+
+        @pl.loop(1, owners)
+        def _(offset):
+            peer = lax.rem(me + offset, owners)
+            copy = block_copy(phase, peer, peer)
+            copy.wait_send()
+            copy.wait_recv()
+
+
+def coarse_exchange(signal, taps, place):
+    _, rows, width = signal.shape
+    chunks = width // LANES
+    owners = lax.axis_size(GROUP)
+    twist, high, low = coarse_tables(width)
+    lead = rows // PHASES
+    blocks = (owners, PHASES, chunks // owners, 2, lead, LANES)
+    return pl.pallas_call(
+        exchange_kernel,
+        out_shape=jax.ShapeDtypeStruct(blocks, jnp.float32),
+        in_specs=[pl.BlockSpec(memory_space=pltpu.VMEM)] * 6,
+        out_specs=pl.BlockSpec(memory_space=pl.ANY),
+        scratch_shapes=[
+            pltpu.VMEM((2, lead, width), jnp.float32),
+            pltpu.VMEM((2, chunks, rows + lead, LANES), jnp.float32),
+            pltpu.VMEM((2, chunks, rows, LANES), jnp.float32),
+            pltpu.VMEM((chunks, rows, 2 * LANES), jnp.float32),
+            pltpu.VMEM((chunks, rows, 2 * LANES), jnp.float32),
+            pltpu.VMEM(blocks, jnp.float32),
+            pltpu.SemaphoreType.DMA,
+            pltpu.SemaphoreType.DMA,
+            pltpu.SemaphoreType.DMA((PHASES, owners)),
+            pltpu.SemaphoreType.DMA((PHASES, owners)),
+            pltpu.SemaphoreType.DMA,
+        ],
+        compiler_params=pltpu.CompilerParams(collective_id=0, has_side_effects=True),
+        name="exchange",
+    )(signal, taps, place, twist, high, low)
+
+
 def fine_kernel(arrived_ref, taps_ref, cos_high, cos_low, sin_high, sin_low, out_ref):
     sources, slot_chunks, _, rows, slots = arrived_ref.shape
     length = sources * rows
@@ -173,7 +301,7 @@
     high, low = [], []
     for c in range(2):
         series = arrived_ref[:, 0, c].reshape(length, slots)
-        filtered = series.T * taps_ref[...]
+        filtered = series.T * taps_ref[0:1, :length]
         parts = split(filtered)
         high.append(parts[0])
         low.append(parts[1])
@@ -209,12 +337,12 @@
         out_shape=jax.ShapeDtypeStruct((2, slot_chunks * slots * per_slot, LANES), jnp.float32),
         in_specs=[
             pl.BlockSpec((sources, 1, 2, rows, slots), lambda i: (0, i, 0, 0, 0)),
-            whole((1, length)),
+            whole(fine_taps.shape),
         ]
         + [whole((length, width))] * 4,
         out_specs=pl.BlockSpec((2, slots * per_slot, LANES), lambda i: (0, i, 0)),
         name="fine",
-    )(arrived, fine_taps[0:1, :length], *tables)
+    )(arrived, fine_taps, *tables)
     return out.reshape(2, 1, slot_chunks * slots, 1, width)
 
 
@@ -245,15 +373,14 @@
     chunks = width // LANES
     owners = lax.axis_size(GROUP)
     own_count = width // owners
-    place = (channel_order % chunks * LANES + channel_order // chunks).reshape(chunks, LANES)
+    place = channel_order.reshape(chunks, LANES)
     lead = -(-(tap_count - 1) // ROWS) * ROWS
+    total_len = owners * slab_len
+    if own_count % LANES == 0 and total_len <= fine_taps.shape[1] and slab_len == PHASES * lead:
+        arrived = coarse_exchange(signal, coarse_taps, place)
+        return fine_local(arrived.reshape(-1, *arrived.shape[2:]), fine_taps)
     next_rows = shifted(signal[:, :lead], GROUP, -1)
     ordered = coarse_local(signal, next_rows, coarse_taps, place)
-    total_len = owners * slab_len
-    if own_count % LANES == 0 and total_len <= fine_taps.shape[1]:
-        blocks = ordered.reshape(owners, own_count // LANES, 2, slab_len, LANES)
-        arrived = lax.all_to_all(blocks, GROUP, split_axis=0, concat_axis=0, tiled=True)
-        return fine_local(arrived, fine_taps)
     blocks = ordered.transpose(0, 3, 1, 2).reshape(owners, own_count, 2, slab_len)
     arrived = lax.all_to_all(blocks, GROUP, split_axis=0, concat_axis=0, tiled=True)
     series = arrived.transpose(2, 1, 0, 3).reshape(2, own_count, total_len)

time: 74.9 us -> 48.6 us (0.65)
  waiting for transfers between devices: 38 us -> 0 us
  Pallas kernels: 23.8 us -> 48.3 us
  starting transfers between devices: 7.22 us -> 0 us
  local copies, waits for them, and re-layouts: 4.11 us -> 0 us
  other arithmetic: 1.34 us -> 0 us
    pallas_call x1, Pallas kernels: 16.7 us -> 41.2 us  [coarse_exchange(): pl.pallas_call(exchange_kernel, out_shape=jax.ShapeDtypeStruct(blocks, jn...]
    all_to_all x1 -> x0, waiting for transfers between devices: 23.9 us -> none  [body(): lax.all_to_all(blocks, GROUP, split_axis=0, concat_axis=0, tiled=True)]
    ppermute x1 -> x0, waiting for transfers between devices: 14.2 us -> none  [shifted(): lax.ppermute(value, axis, [(source, source + steps) for source in range(i...]
    all_to_all x1 -> x0, starting transfers between devices: 5.93 us -> none  [body(): lax.all_to_all(blocks, GROUP, split_axis=0, concat_axis=0, tiled=True)]
    slice x2 -> x0, local copies, waits for them, and re-layouts: 2.35 us -> none  [the longest x1 1.28 us: fine_local(): fine_taps[0:1, :length]]
    unnamed x4 -> x0, local copies, waits for them, and re-layouts: 1.76 us -> none
    reshape x1 -> x0, other arithmetic: 1.34 us -> none  [body(): (channel_order % chunks * LANES + channel_order // chunks).reshape(chunks...]
    ppermute x1 -> x0, starting transfers between devices: 1.29 us -> none  [shifted(): lax.ppermute(value, axis, [(source, source + steps) for source in range(i...]
  transfers between devices with their start and end apart: 2 -> 0, of which waited for: 2 -> 0; matrix products, arithmetic and copies ran while one was open for 4% -> 0% of each run, Pallas kernels for 0% -> 0%
where the time goes in v2:
time: 48.6 us; the launch traced here: 48.3 us
  Pallas kernels  48.3 us (99%)
    pallas_call x1, Pallas kernels, coarse_exchange(): pl.pallas_call(exchange_kernel, out_shape=jax.ShapeDtypeStruct(blocks, jn...  41.2 us
    pallas_call x1, Pallas kernels, fine_local(): pl.pallas_call(fine_kernel, grid=(slot_chunks,), out_shape=jax.ShapeDtype...  7.1 us

profile of v2, /device:TPU:0, one launch (start us, length us, event | category | flops | bytes accessed | tf_op | source)
XLA Modules:
  0.0 48.3 jit_solution(11659232447353157130)
XLA Ops:
  0.0 41.2 %exchange.1 = f32[8,2,4,2,16,128]{5,4,3,2,1,0:T(8,128)} custom-call(f32[2,32,4096]{2,1,0:T(8,128)} %bitcast.5, f32[16,4096]{1,0:T(8,128)} %taps_ref.2, s32[32,128]{1,0:T(8,128)} %bitcast.6, f32[2,32,128]{2,1,0:T(8,128)} %constant.14.clone.twist_ref, bf16[256,256]{1,0:T(8,128)(2,1)} %constant.15.clone.high_ref, bf16[256,256]{1,0:T(8,128)(2,1)} %constant.16.clone.low_ref), custom_call_target="tpu_custom_call" | custom-call | tf_op jit(solution)/shard_map/exchange/pallas_call | solution.py:274
  41.2 7.1 %fine.1 = f32[2,4096,128]{2,1,0:T(8,128)} custom-call(f32[16,4,2,16,128]{4,3,2,1,0:T(8,128)} %bitcast.4, f32[16,1024]{1,0:T(8,128)} %taps_ref.3, bf16[256,1024]{1,0:T(8,128)(2,1)} %constant.17.clone.cos_high, bf16[256,1024]{1,0:T(8,128)(2,1)} %constant.18.clone.cos_low, bf16[256,1024]{1,0:T(8,128)(2,1)} %constant.19.clone.sin_high, ...), custom_call_target="tpu_custom_call" | custom-call | tf_op jit(solution)/shard_map/fine/pallas_call | solution.py:334

commit v3 on v2

--- a/solution.py
+++ b/solution.py
@@ -12,7 +12,6 @@
 LANES = 128
 ROWS = 8
 GROUP = ("tm", "sect")
-PHASES = 2
 
 
 def shifted(value, axis, steps):
@@ -178,8 +177,10 @@
     chunks = spec.shape[0]
     slot_chunks = chunks // owners
     slab_len = signal_ref.shape[1]
-    rows = slab_len // PHASES
-    lead = halo.shape[1]
+    rows = ROWS
+    phases = slab_len // rows
+    reach = taps_ref.shape[0] - 1
+    parts = halo.shape[0]
 
     def device(index):
         return {"tm": lax.div(index, sects), "sect": lax.rem(index, sects)}
@@ -190,18 +191,20 @@
         pl.semaphore_signal(barrier, inc=1, device_id=device(peer), device_id_type=pl.DeviceIdType.MESH)
     pl.semaphore_wait(barrier, owners - 1)
 
-    halo_copy = pltpu.make_async_remote_copy(
-        src_ref=signal_ref.at[:, 0:lead, :],
-        dst_ref=halo,
-        send_sem=halo_send,
-        recv_sem=halo_recv,
-        device_id=device(lax.rem(me + owners - 1, owners)),
-        device_id_type=pl.DeviceIdType.MESH,
-    )
+    def halo_copy(part):
+        return pltpu.make_async_remote_copy(
+            src_ref=signal_ref.at[:, part * ROWS : (part + 1) * ROWS, :],
+            dst_ref=halo.at[part],
+            send_sem=halo_send.at[part],
+            recv_sem=halo_recv.at[part],
+            device_id=device(lax.rem(me + owners - 1, owners)),
+            device_id_type=pl.DeviceIdType.MESH,
+        )
 
     @pl.when(me > 0)
     def _():
-        halo_copy.start()
+        for part in range(parts):
+            halo_copy(part).start()
 
     def block_copy(phase, owner, source):
         return pltpu.make_async_remote_copy(
@@ -214,27 +217,36 @@
         )
 
     fill(ext, signal_ref, 0)
-    for phase in range(PHASES):
+    taken = 0
+    for phase in range(phases):
         start = phase * rows
-        if phase == PHASES - 1:
+        needed = -(-(start + rows + reach - slab_len) // ROWS)
+        for part in range(taken, needed):
+            at = slab_len + part * ROWS
 
             @pl.when(me < owners - 1)
             def _():
-                halo_copy.wait_recv()
-                fill(ext, halo, slab_len)
+                halo_copy(part).wait_recv()
+                fill(ext, halo.at[part], at)
 
             @pl.when(me == owners - 1)
             def _():
-                ext[:, :, slab_len:, :] = jnp.zeros((2, chunks, lead, LANES), jnp.float32)
-
+                ext[:, :, at : at + ROWS, :] = jnp.zeros((2, chunks, ROWS, LANES), jnp.float32)
+
+        taken = max(taken, needed)
         spectra_rows(ext, taps_ref, twist_ref, high_ref, low_ref, filt, lhs, spec, start, rows)
 
         @pl.loop(0, owners)
         def _(step):
-            turn = lax.div(step, sects)
             half = tms // 2
+            if phase < phases - parts:
+                turn = lax.rem(step, tms)
+                to_sect = lax.rem(sect + lax.div(step, tms), sects)
+            else:
+                turn = lax.div(step, sects)
+                to_sect = lax.rem(sect + 1 + step, sects)
             turn = jnp.where(turn < tms - half, half + turn, tms - 1 - turn)
-            owner = lax.rem(tm + turn, tms) * sects + lax.rem(sect + 1 + step, sects)
+            owner = lax.rem(tm + turn, tms) * sects + to_sect
 
             @pl.loop(0, slot_chunks)
             def _(i):
@@ -252,9 +264,10 @@
 
     @pl.when(me > 0)
     def _():
-        halo_copy.wait_send()
-
-    for phase in range(PHASES):
+        for part in range(parts):
+            halo_copy(part).wait_send()
+
+    for phase in range(phases):
 
         @pl.loop(1, owners)
         def _(offset):
@@ -269,24 +282,25 @@
     chunks = width // LANES
     owners = lax.axis_size(GROUP)
     twist, high, low = coarse_tables(width)
-    lead = rows // PHASES
-    blocks = (owners, PHASES, chunks // owners, 2, lead, LANES)
+    parts = -(-(taps.shape[0] - 1) // ROWS)
+    phases = rows // ROWS
+    blocks = (owners, phases, chunks // owners, 2, ROWS, LANES)
     return pl.pallas_call(
         exchange_kernel,
         out_shape=jax.ShapeDtypeStruct(blocks, jnp.float32),
         in_specs=[pl.BlockSpec(memory_space=pltpu.VMEM)] * 6,
         out_specs=pl.BlockSpec(memory_space=pl.ANY),
         scratch_shapes=[
-            pltpu.VMEM((2, lead, width), jnp.float32),
-            pltpu.VMEM((2, chunks, rows + lead, LANES), jnp.float32),
+            pltpu.VMEM((parts, 2, ROWS, width), jnp.float32),
+            pltpu.VMEM((2, chunks, rows + parts * ROWS, LANES), jnp.float32),
             pltpu.VMEM((2, chunks, rows, LANES), jnp.float32),
             pltpu.VMEM((chunks, rows, 2 * LANES), jnp.float32),
             pltpu.VMEM((chunks, rows, 2 * LANES), jnp.float32),
             pltpu.VMEM(blocks, jnp.float32),
-            pltpu.SemaphoreType.DMA,
-            pltpu.SemaphoreType.DMA,
-            pltpu.SemaphoreType.DMA((PHASES, owners)),
-            pltpu.SemaphoreType.DMA((PHASES, owners)),
+            pltpu.SemaphoreType.DMA((parts,)),
+            pltpu.SemaphoreType.DMA((parts,)),
+            pltpu.SemaphoreType.DMA((phases, owners)),
+            pltpu.SemaphoreType.DMA((phases, owners)),
             pltpu.SemaphoreType.DMA,
         ],
         compiler_params=pltpu.CompilerParams(collective_id=0, has_side_effects=True),
@@ -376,7 +390,7 @@
     place = channel_order.reshape(chunks, LANES)
     lead = -(-(tap_count - 1) // ROWS) * ROWS
     total_len = owners * slab_len
-    if own_count % LANES == 0 and total_len <= fine_taps.shape[1] and slab_len == PHASES * lead:
+    if own_count % LANES == 0 and total_len <= fine_taps.shape[1] and slab_len % ROWS == 0 and lead <= slab_len:
         arrived = coarse_exchange(signal, coarse_taps, place)
         return fine_local(arrived.reshape(-1, *arrived.shape[2:]), fine_taps)
     next_rows = shifted(signal[:, :lead], GROUP, -1)

time: 48.6 us -> 50.2 us (1.033)
  Pallas kernels: 48.3 us -> 49.9 us
    pallas_call x1, Pallas kernels: 41.2 us -> 42.8 us  [coarse_exchange(): pl.pallas_call(exchange_kernel, out_shape=jax.ShapeDtypeStruct(blocks, jn...]
where the time goes in v3:
time: 50.2 us; the launch traced here: 49.9 us
  Pallas kernels  49.9 us (99%)
    pallas_call x1, Pallas kernels, coarse_exchange(): pl.pallas_call(exchange_kernel, out_shape=jax.ShapeDtypeStruct(blocks, jn...  42.8 us
    pallas_call x1, Pallas kernels, fine_local(): pl.pallas_call(fine_kernel, grid=(slot_chunks,), out_shape=jax.ShapeDtype...  7.11 us

profile of v3, /device:TPU:0, one launch (start us, length us, event | category | flops | bytes accessed | tf_op | source)
XLA Modules:
  0.0 49.9 jit_solution(16120902814937488495)
XLA Ops:
  0.0 42.8 %exchange.1 = f32[8,4,4,2,8,128]{5,4,3,2,1,0:T(8,128)} custom-call(f32[2,32,4096]{2,1,0:T(8,128)} %bitcast.5, f32[16,4096]{1,0:T(8,128)} %taps_ref.2, s32[32,128]{1,0:T(8,128)} %bitcast.6, f32[2,32,128]{2,1,0:T(8,128)} %constant.14.clone.twist_ref, bf16[256,256]{1,0:T(8,128)(2,1)} %constant.15.clone.high_ref, bf16[256,256]{1,0:T(8,128)(2,1)} %constant.16.clone.low_ref), custom_call_target="tpu_custom_call" | custom-call | tf_op jit(solution)/shard_map/exchange/pallas_call | solution.py:288
  42.8 7.1 %fine.1 = f32[2,4096,128]{2,1,0:T(8,128)} custom-call(f32[32,4,2,8,128]{4,3,2,1,0:T(8,128)} %bitcast.4, f32[16,1024]{1,0:T(8,128)} %taps_ref.3, bf16[256,1024]{1,0:T(8,128)(2,1)} %constant.17.clone.cos_high, bf16[256,1024]{1,0:T(8,128)(2,1)} %constant.18.clone.cos_low, bf16[256,1024]{1,0:T(8,128)(2,1)} %constant.19.clone.sin_high, ...), custom_call_target="tpu_custom_call" | custom-call | tf_op jit(solution)/shard_map/fine/pallas_call | solution.py:348

commit v4 on v2

--- a/solution.py
+++ b/solution.py
@@ -294,53 +294,58 @@
     )(signal, taps, place, twist, high, low)
 
 
-def fine_kernel(arrived_ref, taps_ref, cos_high, cos_low, sin_high, sin_low, out_ref):
+def fine_kernel(arrived_ref, taps_ref, even_high, even_low, odd_high, odd_low, out_ref, series):
     sources, slot_chunks, _, rows, slots = arrived_ref.shape
     length = sources * rows
-    width = cos_high.shape[1]
-    high, low = [], []
+    half = even_high.shape[1] // 2
+    per_slot = 2 * half // LANES
+    taps = taps_ref[:, :length].T[:, 0:1]
+    for i in range(slot_chunks):
+        for c in range(2):
+            series[i, c] = arrived_ref[:, i, c].reshape(length, slots) * taps
+    sums = []
+    for parity, (table_high, table_low) in enumerate(((even_high, even_low), (odd_high, odd_low))):
+        at = pl.ds(parity, length // 2, stride=2)
+        value = jnp.concatenate(
+            [jnp.concatenate([series[i, c, at, :].T for c in range(2)], axis=1) for i in range(slot_chunks)], axis=0
+        )
+        high, low = split(value)
+        product = partial(jnp.dot, preferred_element_type=jnp.float32)
+        both = product(jnp.concatenate([high, low], axis=0), table_high[...])
+        count = slot_chunks * slots
+        sums.append(both[:count] + (both[count:] + product(high, table_low[...])))
     for c in range(2):
-        series = arrived_ref[:, 0, c].reshape(length, slots)
-        filtered = series.T * taps_ref[0:1, :length]
-        parts = split(filtered)
-        high.append(parts[0])
-        low.append(parts[1])
-    high = jnp.concatenate(high, axis=0)
-    low = jnp.concatenate(low, axis=0)
-    per_slot = width // LANES
-    step = 2 * LANES
-    for m in range(width // step):
-        lanes = slice(m * step, (m + 1) * step)
-        with_cos = dot3(high, low, cos_high[:, lanes], cos_low[:, lanes])
-        with_sin = dot3(high, low, sin_high[:, lanes], sin_low[:, lanes])
-        re = with_cos[:slots] + with_sin[slots:]
-        im = with_cos[slots:] - with_sin[:slots]
-        for h in range(2):
-            at = pl.ds(m * 2 + h, slots, stride=per_slot)
-            out_ref[0, at, :] = re[:, h * LANES : (h + 1) * LANES]
-            out_ref[1, at, :] = im[:, h * LANES : (h + 1) * LANES]
+        for h in range(half // LANES):
+            lanes = slice(c * half + h * LANES, c * half + (h + 1) * LANES)
+            even, odd = sums[0][:, lanes], sums[1][:, lanes]
+            out_ref[c, pl.ds(h, slot_chunks * slots, stride=per_slot), :] = even + odd
+            out_ref[c, pl.ds(h + half // LANES, slot_chunks * slots, stride=per_slot), :] = even - odd
 
 
 def fine_local(arrived, fine_taps):
     sources, slot_chunks, _, rows, slots = arrived.shape
     length = sources * rows
     width = fine_taps.shape[1]
-    j, m = np.arange(length)[:, None], np.arange(width)[None, :]
-    angle = 2.0 * np.pi * (j * m % width) / width
-    scale = 1.0 / math.sqrt(width)
-    tables = split_const(np.cos(angle) * scale) + split_const(np.sin(angle) * scale)
+    tables = []
+    for parity in range(2):
+        j, m = np.arange(parity, length, 2)[:, None], np.arange(width // 2)[None, :]
+        angle = 2.0 * np.pi * (j * m % width) / width
+        cos, sin = np.cos(angle), np.sin(angle)
+        tables += split_const(np.block([[cos, -sin], [sin, cos]]) / math.sqrt(width))
     per_slot = width // LANES
+    step = 2 if slot_chunks % 2 == 0 else 1
     whole = lambda shape: pl.BlockSpec(shape, lambda i: (0, 0))
     out = pl.pallas_call(
         fine_kernel,
-        grid=(slot_chunks,),
+        grid=(slot_chunks // step,),
         out_shape=jax.ShapeDtypeStruct((2, slot_chunks * slots * per_slot, LANES), jnp.float32),
         in_specs=[
-            pl.BlockSpec((sources, 1, 2, rows, slots), lambda i: (0, i, 0, 0, 0)),
+            pl.BlockSpec((sources, step, 2, rows, slots), lambda i: (0, i, 0, 0, 0)),
             whole(fine_taps.shape),
         ]
         + [whole((length, width))] * 4,
-        out_specs=pl.BlockSpec((2, slots * per_slot, LANES), lambda i: (0, i, 0)),
+        out_specs=pl.BlockSpec((2, step * slots * per_slot, LANES), lambda i: (0, i, 0)),
+        scratch_shapes=[pltpu.VMEM((step, 2, length, slots), jnp.float32)],
         name="fine",
     )(arrived, fine_taps, *tables)
     return out.reshape(2, 1, slot_chunks * slots, 1, width)

time: 48.6 us -> 47.2 us (0.971)
  Pallas kernels: 48.3 us -> 47.1 us
    pallas_call x1, Pallas kernels: 7.1 us -> 5.83 us  [fine_local(): pl.pallas_call(fine_kernel, grid=(slot_chunks // step,), out_shape=jax.Sh...]
where the time goes in v4:
time: 47.2 us; the launch traced here: 47.1 us
  Pallas kernels  47.1 us (100%)
    pallas_call x1, Pallas kernels, coarse_exchange(): pl.pallas_call(exchange_kernel, out_shape=jax.ShapeDtypeStruct(blocks, jn...  41.2 us
    pallas_call x1, Pallas kernels, fine_local(): pl.pallas_call(fine_kernel, grid=(slot_chunks // step,), out_shape=jax.Sh...  5.83 us

profile of v4, /device:TPU:0, one launch (start us, length us, event | category | flops | bytes accessed | tf_op | source)
XLA Modules:
  0.0 47.1 jit_solution(5767715971875989301)
XLA Ops:
  0.0 41.2 %exchange.1 = f32[8,2,4,2,16,128]{5,4,3,2,1,0:T(8,128)} custom-call(f32[2,32,4096]{2,1,0:T(8,128)} %bitcast.5, f32[16,4096]{1,0:T(8,128)} %taps_ref.2, s32[32,128]{1,0:T(8,128)} %bitcast.6, f32[2,32,128]{2,1,0:T(8,128)} %constant.14.clone.twist_ref, bf16[256,256]{1,0:T(8,128)(2,1)} %constant.15.clone.high_ref, bf16[256,256]{1,0:T(8,128)(2,1)} %constant.16.clone.low_ref), custom_call_target="tpu_custom_call" | custom-call | tf_op jit(solution)/shard_map/exchange/pallas_call | solution.py:274
  41.2 5.8 %fine.1 = f32[2,4096,128]{2,1,0:T(8,128)} custom-call(f32[16,4,2,16,128]{4,3,2,1,0:T(8,128)} %bitcast.4, f32[16,1024]{1,0:T(8,128)} %taps_ref.3, bf16[256,1024]{1,0:T(8,128)(2,1)} %constant.17.clone.even_high, bf16[256,1024]{1,0:T(8,128)(2,1)} %constant.18.clone.even_low, bf16[256,1024]{1,0:T(8,128)(2,1)} %constant.19.clone.odd_high, ...), custom_call_target="tpu_custom_call" | custom-call | tf_op jit(solution)/shard_map/fine/pallas_call | solution.py:338
